TPU v7x, 1024 devices: a whole 8x8x8 slice. The times are simulated.
1024 devices in a mesh: dp: 16 (over y, core), tensor: 8 (over x), pipe: 8 (over z).
Axes of the slice: x: 8, y: 8, z: 8, core: 2. Of those that a mesh axis runs over, the one named last changes fastest.
Arguments:
- grad_parts: float32 [16, 8, 8, 64, 8192], P('dp', 'pipe', 'tensor'), may hold values from -24 to 24
- drop_flags: int32 [16, 8, 8, 64], P('dp', 'pipe', 'tensor'), may hold values from 0 to 1, as said below
- owner_order: int32 [16], replicated, may hold values from 0 to 15, each once
- step_count: int32 [], replicated, may hold values from 1 to 11
- master: float32 [8, 8, 64, 8192], P('pipe', 'tensor', None, 'dp'), may hold values from -6 to 6
- moment_m: float32 [8, 8, 64, 8192], P('pipe', 'tensor', None, 'dp'), may hold values from -0.15625 to 0.15625
- moment_v: float32 [8, 8, 64, 8192], P('pipe', 'tensor', None, 'dp'), may hold values from 0.0001 to 0.001
Outputs:
- new_master: float32 [8, 8, 64, 8192], P('pipe', 'tensor', None, 'dp')
- new_m: float32 [8, 8, 64, 8192], P('pipe', 'tensor', None, 'dp')
- new_v: float32 [8, 8, 64, 8192], P('pipe', 'tensor', None, 'dp')
- direction: float32 [8, 8, 64, 8192], P('pipe', 'tensor', None, 'dp')
- dropped_total: int32 [], replicated
Inputs may be any that keep to these rules, and one draw needn't show every extreme that they name: `drop_flags`: A row may be flagged by every replica.
All inputs are finite; a program needn't handle non-finite values.
Results may differ from a plain program's by a relative error of at most 0.0003.
Values sent between devices are 32-bit elements; how exact they have to be, the bound alone decides.
A program may use at most 32 MiB of HBM per device.

v0:
```python
import jax
import jax.numpy as jnp
from jax import lax
from jax.sharding import Mesh
from jax.sharding import PartitionSpec as P

DP = ("dp_0", "dp_1")
DP_TENSOR_PIPE = ("dp_0", "dp_1", "tensor", "pipe")


def cut_along(array, dim, peers):
    before, after = (array.shape[:dim], array.shape[dim + 1 :])
    return jnp.moveaxis(array.reshape(*before, peers, -1, *after), dim, 0)


def sent_and_summed(array, axis, dim):
    blocks = cut_along(array, dim, lax.axis_size(axis))
    arrived = lax.all_to_all(blocks, axis, split_axis=0, concat_axis=0, tiled=True)
    return arrived.sum(axis=0)


def from_everyone(array, axis):
    peers = lax.axis_size(axis)
    return lax.all_to_all(
        jnp.broadcast_to(array[None], (peers, *array.shape)), axis, 0, 0, tiled=True
    )


def taken_together(array, axis):
    everything = from_everyone(array, axis)
    return jnp.sum(everything, axis=0)


def one_axis_at_a_time(array, axes):
    for axis in axes:
        array = lax.psum(array, axis)
    return array


def body(grad_parts, drop_flags, owner_order, step_count, master, moment_m, moment_v):
    replicas = lax.axis_size(DP)
    flags = drop_flags[0, 0, 0]
    kept = (1 - flags).astype(jnp.float32)
    local_grad = grad_parts[0, 0, 0]
    rows_here = local_grad.shape[0]
    width = local_grad.shape[1]
    block_cols = width // replicas
    term = local_grad * kept[:, None]
    blocks = jnp.take(term.reshape(rows_here, replicas, block_cols), owner_order, axis=1)
    summed = sent_and_summed(blocks.reshape(rows_here, width), DP, 1)
    count = taken_together(kept, DP)
    grad = summed / jnp.maximum(count, 1.0)[:, None]
    square_sum, dropped = (
        one_axis_at_a_time(jnp.sum(grad * grad), DP_TENSOR_PIPE),
        one_axis_at_a_time(jnp.sum(flags).astype(jnp.float32), DP_TENSOR_PIPE),
    )
    entries = rows_here * width * lax.axis_size("tensor") * lax.axis_size("pipe")
    rms = jnp.sqrt(square_sum / entries)
    clip = jnp.minimum(1.0, 0.05 / (rms + 1e-06))
    scaled = clip * grad
    old_m = moment_m[0, 0]
    old_v = moment_v[0, 0]
    weights = master[0, 0]
    new_m = 0.9 * old_m + 0.1 * scaled
    new_v = 0.999 * old_v + 0.001 * scaled * scaled
    steps = step_count.astype(jnp.float32)
    m_hat = new_m / (1.0 - jnp.power(0.9, steps))
    v_hat = new_v / (1.0 - jnp.power(0.999, steps))
    direction = m_hat / (jnp.sqrt(v_hat) + 1e-08) + 0.1 * weights
    new_master = weights - 0.001 * direction
    return (
        new_master[None, None],
        new_m[None, None],
        new_v[None, None],
        direction[None, None],
        dropped.astype(jnp.int32),
    )


def solution(mesh):
    finer = Mesh(
        mesh.devices.reshape(8, 2, mesh.shape["tensor"], mesh.shape["pipe"]),
        ("dp_0", "dp_1", "tensor", "pipe"),
    )
    placed = (
        P(DP, "pipe", "tensor", None, None),
        P(DP, "pipe", "tensor", None),
        P(),
        P(),
        P("pipe", "tensor", None, DP),
        P("pipe", "tensor", None, DP),
        P("pipe", "tensor", None, DP),
    )
    return jax.shard_map(
        body,
        mesh=finer,
        in_specs=placed,
        out_specs=(
            P("pipe", "tensor", None, DP),
            P("pipe", "tensor", None, DP),
            P("pipe", "tensor", None, DP),
            P("pipe", "tensor", None, DP),
            P(),
        ),
        check_vma=False,
    )
```

profile of v0, /device:TPU:16, one launch (start us, length us, event | category | flops | bytes accessed | tf_op | source)
XLA Modules:
  0.0 147.7 jit_solution(13686131545010351468)
XLA Ops:
  0.6 1.3 fusion.3
  1.9 0.6 broadcast_in_dim.27
  2.5 16.2 %all-to-all-start.1 = ((f32[16,1,64]{2,1,0:T(1,128)}), f32[16,1,64]{2,1,0:T(1,128)S(1)}, u32[]{:S(2)}, u32[]{:S(2)}) async-start(f32[16,1,64]{2,1,0:T(1,128)} %broadcast_in_dim.27), calls=%async_computation.1 | async-start | bytes 16384 | tf_op jit(solution)/shard_map/all_to_all | solution.py:24
  18.8 0.7 compare_select_fusion
  19.4 0.7 compare_and_fusion
  20.1 2.8 %copy.16 = f32[8,8,16,512]{3,2,1,0:T(8,128)S(1)} copy(f32[8,8,16,512]{3,1,2,0:T(8,128)} %bitcast.18) | data formatting | bytes 4194304
  22.9 1.2 copy_multiply_fusion
  24.1 2.0 %gather_fusion = f32[16,64,512]{2,1,0:T(8,128)} fusion(f32[64,16,512]{2,0,1:T(8,128)S(1)} %copy_multiply_fusion, s32[1024]{0:T(1024)S(1)} %pad_clamp_fusion), kind=kCustom, calls=%fused_computation | custom fusion | bytes 4194368 | tf_op jit(solution)/shard_map/jit(_take)/gather | solution.py:49
  26.1 3.3 %broadcast_select_fusion = f32[16,64,512]{2,1,0:T(8,128)} fusion(f32[16,64,512]{2,1,0:T(8,128)} %gather_fusion, pred[16]{0:T(512)(128)(4,1)S(1)} %compare_and_fusion), kind=kLoop, calls=%fused_computation.2 | loop fusion | flops 524288 | bytes 4194320 | tf_op jit(solution)/shard_map/jit(_take)/select_n | solution.py:49
  29.5 0.0 all-to-all-done.1
  29.5 7.3 %all-to-all-start = ((f32[16,64,512]{2,1,0:T(8,128)}), f32[16,64,512]{2,1,0:T(8,128)S(1)}, u32[]{:S(2)}, u32[]{:S(2)}) async-start(f32[16,64,512]{2,1,0:T(8,128)} %broadcast_select_fusion), calls=%async_computation | async-start | bytes 4194304 | tf_op jit(solution)/shard_map/all_to_all | solution.py:18
  36.7 0.0 copy-start
  36.7 0.0 copy-start.1
  36.7 0.0 copy-start.2
  38.2 45.7 %all-to-all-done = f32[16,64,512]{2,1,0:T(8,128)S(1)} async-done(((f32[16,64,512]{2,1,0:T(8,128)}), f32[16,64,512]{2,1,0:T(8,128)S(1)}, u32[]{:S(2)}, u32[]{:S(2)}) %all-to-all-start) | async-done | bytes 2097184 | tf_op jit(solution)/shard_map/all_to_all | solution.py:18
  83.9 0.2 reduce_sum.38
  84.1 0.7 multiply_reduce_fusion
  84.8 16.9 %all-reduce.2 = (f32[]{:T(128)}, f32[]{:T(128)}) all-reduce(f32[]{:T(128)} %multiply_reduce_fusion, f32[]{:T(128)S(6)} %convert_element_type.26), channel_id=1, replica_groups=mesh['dp_0'=8,'dp_1'=2,'tensor'=8,'pipe'=8] {'dp_0'}, use_global_device_ids=true, to_apply=%region_3.4 | all-reduce | flops 2 | bytes 16 | tf_op jit(solution)/shard_map/psum | solution.py:36
  101.7 3.1 %all-reduce.3 = (f32[]{:T(128)}, f32[]{:T(128)}) all-reduce(f32[]{:T(128)} %get-tuple-element.9, f32[]{:T(128)} %get-tuple-element.10), channel_id=1, replica_groups=mesh['dp_0'=8,'dp_1'=2,'tensor'=8,'pipe'=8] {'dp_1'}, use_global_device_ids=true, to_apply=%region_4.5 | all-reduce | flops 2 | bytes 16 | tf_op jit(solution)/shard_map/psum | solution.py:36
  104.8 14.8 %all-reduce.1 = (f32[]{:T(128)}, f32[]{:T(128)}) all-reduce(f32[]{:T(128)} %get-tuple-element.11, f32[]{:T(128)} %get-tuple-element.12), channel_id=1, replica_groups=mesh['dp_0'=8,'dp_1'=2,'tensor'=8,'pipe'=8] {'tensor'}, use_global_device_ids=true, to_apply=%region_5.6 | all-reduce | flops 2 | bytes 16 | tf_op jit(solution)/shard_map/psum | solution.py:36
  119.6 24.7 %all-reduce = (f32[]{:T(128)}, f32[]{:T(128)}) all-reduce(f32[]{:T(128)} %get-tuple-element.7, f32[]{:T(128)} %get-tuple-element.8), channel_id=1, replica_groups=mesh['dp_0'=8,'dp_1'=2,'tensor'=8,'pipe'=8] {'pipe'}, use_global_device_ids=true, to_apply=%region_6.7 | all-reduce | flops 2 | bytes 16 | tf_op jit(solution)/shard_map/psum | solution.py:36
  145.6 0.0 copy-done
  145.6 0.0 copy-done.1
  145.6 0.0 copy-done.2
  145.6 1.0 multiply_subtract_fusion
  (3 shorter events, 0.0 us)
Async XLA Ops:
  2.5 26.9 %all-to-all-start.1 = ((f32[16,1,64]{2,1,0:T(1,128)}), f32[16,1,64]{2,1,0:T(1,128)S(1)}, u32[]{:S(2)}, u32[]{:S(2)}) async-start(f32[16,1,64]{2,1,0:T(1,128)} %broadcast_in_dim.27), calls=%async_computation.1 | async-start | bytes 16384 | tf_op jit(solution)/shard_map/all_to_all | solution.py:24
  29.5 54.5 %all-to-all-start = ((f32[16,64,512]{2,1,0:T(8,128)}), f32[16,64,512]{2,1,0:T(8,128)S(1)}, u32[]{:S(2)}, u32[]{:S(2)}) async-start(f32[16,64,512]{2,1,0:T(8,128)} %broadcast_select_fusion), calls=%async_computation | async-start | bytes 4194304 | tf_op jit(solution)/shard_map/all_to_all | solution.py:18
  36.7 108.9 %copy-start = (f32[1,1,64,512]{3,2,1,0:T(8,128)S(1)}, f32[1,1,64,512]{3,2,1,0:T(8,128)}, u32[]{:S(2)}) copy-start(f32[1,1,64,512]{3,2,1,0:T(8,128)} %param.11) | copy-start | bytes 393220
  36.7 108.9 %copy-start.1 = (f32[1,1,64,512]{3,2,1,0:T(8,128)S(1)}, f32[1,1,64,512]{3,2,1,0:T(8,128)}, u32[]{:S(2)}) copy-start(f32[1,1,64,512]{3,2,1,0:T(8,128)} %param.13) | copy-start | bytes 393220
  36.7 108.9 %copy-start.2 = (f32[1,1,64,512]{3,2,1,0:T(8,128)S(1)}, f32[1,1,64,512]{3,2,1,0:T(8,128)}, u32[]{:S(2)}) copy-start(f32[1,1,64,512]{3,2,1,0:T(8,128)} %param.12) | copy-start | bytes 393220
where the time goes:
time: 148 us
  blocking collectives  59.4 us (40%)
  waiting for transfers between devices  45.7 us (31%)
  starting transfers between devices  23.5 us (16%)
  other arithmetic  9.01 us (6%)
  local copies, waits for them, and re-layouts  5.44 us (4%)
  between operations  4.65 us (3%)
    psum x4, blocking collectives, one_axis_at_a_time(): array = lax.psum(array, axis)  59.4 us
    all_to_all x1, waiting for transfers between devices, sent_and_summed(): lax.all_to_all(blocks, axis, split_axis=0, concat_axis=0, tiled=True)  45.7 us
    all_to_all x1, starting transfers between devices, from_everyone(): lax.all_to_all(jnp.broadcast_to(array[None], (peers, *array.shape)), axis...  16.2 us
    all_to_all x1, starting transfers between devices, sent_and_summed(): lax.all_to_all(blocks, axis, split_axis=0, concat_axis=0, tiled=True)  7.26 us
    select_n x2, other arithmetic, body(): jnp.take(term.reshape(rows_here, replicas, block_cols), owner_order, axis=1)  3.98 us
  transfers between devices with their start and end apart: 2, of which 1 were waited for; matrix products, arithmetic and copies ran while one was open for 7% of the time, Pallas kernels for 0%

commit v1 on v0

v1 whole, which is shorter than its diff:
```python
import jax
import jax.numpy as jnp
from jax import lax
from jax.experimental import pallas as pl
from jax.experimental.pallas import tpu as pltpu
from jax.sharding import Mesh
from jax.sharding import PartitionSpec as P

MESH = pl.DeviceIdType.MESH
Y = 8
ROWS, COLS = 64, 512
WIDTH = 2 * Y * COLS
HALF = ROWS // 2
ENTRIES = 33554432.0

D_ORDER = (4, 3, 5, 2, 6, 1, 7, 0)
UP = ((4, 0), (3, 1), (3, 0), (2, 1), (2, 0), (1, 1), (1, 0))
DOWN = ((4, 1), (3, 0), (3, 1), (2, 0), (2, 1), (1, 0), (1, 1))


def kernel(
    order, steps, flags, grad, master, moment_m, moment_v,
    out_w, out_m, out_v, out_d, out_drop,
    order_s, steps_s, flags_v, x, st, dsend, drecv, ring_send, ring_recv, fsend, frecv, csend, crecv, nsend, nrecv,
    load_sem, small_sem, st_sem, d_ss, d_rs, r_ss, r_rs, f_ss, f_rs, c_ss, c_rs, n_ss, n_rs,
):
    y = lax.axis_index("y")
    c = lax.axis_index("c")
    tx = lax.axis_index("tensor")
    pz = lax.axis_index("pipe")
    other = 1 - c

    barrier = pltpu.get_barrier_semaphore()
    pl.semaphore_signal(barrier, inc=1, device_id={"c": other}, device_id_type=MESH)
    for o in range(1, 8):
        pl.semaphore_signal(barrier, inc=1, device_id={"y": lax.rem(y + o, 8)}, device_id_type=MESH)
        pl.semaphore_signal(barrier, inc=1, device_id={"tensor": lax.rem(tx + o, 8)}, device_id_type=MESH)
        pl.semaphore_signal(barrier, inc=1, device_id={"pipe": lax.rem(pz + o, 8)}, device_id_type=MESH)

    smalls = [
        pltpu.make_async_copy(ref, to, small_sem.at[i])
        for i, (ref, to) in enumerate(((flags, flags_v), (order, order_s), (steps, steps_s)))
    ]
    for s in smalls:
        s.start()
    loads = [
        pltpu.make_async_copy(grad.at[:, pl.ds(b * COLS, COLS)], x.at[b], load_sem.at[b])
        for b in range(2 * Y)
    ]
    for s in loads:
        s.start()
    states = [
        pltpu.make_async_copy(ref, st.at[i], st_sem.at[i])
        for i, ref in enumerate((master, moment_m, moment_v))
    ]
    for s in states:
        s.start()

    for s in smalls:
        s.wait()
    flag_row = flags_v[...].astype(jnp.float32)
    kept_row = 1.0 - flag_row
    eye = lax.broadcasted_iota(jnp.int32, (ROWS, ROWS), 0) == lax.broadcasted_iota(
        jnp.int32, (ROWS, ROWS), 1
    )

    def as_column(row):
        return jnp.sum(jnp.where(eye, jnp.broadcast_to(row, (ROWS, ROWS)), 0.0), axis=1, keepdims=True)

    kept = as_column(kept_row)
    fsend[...] = jnp.concatenate([kept_row, jnp.zeros((1, 128 - ROWS), jnp.float32)], axis=1)

    def mine(chip, core, lo, n):
        return x[order_s[2 * chip + core], lo : lo + n] * kept[lo : lo + n]

    for s in loads:
        s.wait()
    pl.semaphore_wait(barrier, 22)

    d_copies = {}
    for d in D_ORDER:
        chip = lax.rem(y + d, 8)
        dsend[d] = mine(chip, other, 0, ROWS)
        cp = pltpu.make_async_remote_copy(
            src_ref=dsend.at[d], dst_ref=drecv.at[d], send_sem=d_ss.at[d], recv_sem=d_rs.at[d],
            device_id={"c": other}, device_id_type=MESH,
        )
        cp.start()
        d_copies[d] = cp
    f_copy = pltpu.make_async_remote_copy(
        src_ref=fsend, dst_ref=frecv, send_sem=f_ss, recv_sem=f_rs,
        device_id={"c": other}, device_id_type=MESH,
    )
    f_copy.start()

    def on_chip(d, half):
        chip = lax.rem(y + d, 8)
        lo = half * HALF
        return mine(chip, c, lo, HALF) + drecv[d, lo : lo + HALF]

    seen = set()
    sends = []
    waited = set()

    def ring_copy(way, k, half):
        lo = half * HALF
        i = (way * 4 + (k - 1)) * 2 + half
        to = lax.rem(y + (1 if way == 0 else 7), 8)
        return pltpu.make_async_remote_copy(
            src_ref=ring_send.at[way, k - 1, pl.ds(lo, HALF)],
            dst_ref=ring_recv.at[way, k - 1, pl.ds(lo, HALF)],
            send_sem=r_ss.at[i], recv_sem=r_rs.at[i],
            device_id={"y": to}, device_id_type=MESH,
        )

    def stage(way, k, half):
        d = k if way == 0 else 8 - k
        if d not in seen:
            d_copies[d].wait_recv()
            seen.add(d)
        lo = half * HALF
        value = on_chip(d, half)
        top = 4 if half == way else 3
        if k < top:
            ring_copy(way, k + 1, half).wait_recv()
            value = value + ring_recv[way, k, lo : lo + HALF]
        ring_send[way, k - 1, lo : lo + HALF] = value
        cp = ring_copy(way, k, half)
        cp.start()
        sends.append(cp)

    c_copies = []
    for i in range(7):
        stage(0, *UP[i])
        stage(1, *DOWN[i])
        if i == 1:
            f_copy.wait_recv()
            csend[...] = fsend[...] + frecv[...]
            for o in range(1, 8):
                cp = pltpu.make_async_remote_copy(
                    src_ref=csend, dst_ref=crecv.at[o], send_sem=c_ss.at[o], recv_sem=c_rs.at[o],
                    device_id={"y": lax.rem(y + o, 8)}, device_id_type=MESH,
                )
                cp.start()
                c_copies.append(cp)

    for cp in c_copies:
        cp.wait_recv()
    count_row = csend[...]
    for o in range(1, 8):
        count_row = count_row + crecv[o]
    count = jnp.maximum(as_column(count_row[:, :ROWS]), 1.0)

    d_copies[0].wait_recv()
    squares = jnp.zeros((8, COLS), jnp.float32)
    means = []
    for half in (1, 0):
        lo = half * HALF
        part = on_chip(0, half)
        for way in ((0, 1) if half else (1, 0)):
            ring_copy(way, 1, half).wait_recv()
            part = part + ring_recv[way, 0, lo : lo + HALF]
        mean = part / count[lo : lo + HALF]
        means.append(mean)
        sq = mean * mean
        for r in range(0, HALF, 8):
            squares = squares + sq[r : r + 8]
    mean = jnp.concatenate([means[1], means[0]], axis=0)
    squares = squares[:, 0:128] + squares[:, 128:256] + squares[:, 256:384] + squares[:, 384:512]
    squares = jnp.sum(squares, axis=0, keepdims=True)

    message = jnp.concatenate(
        [squares, jnp.concatenate([flag_row, jnp.zeros((1, 128 - ROWS), jnp.float32)], axis=1)], axis=0
    )

    def exchange(phase, peers, message):
        nsend[phase] = message
        copies = []
        for o, peer in peers:
            cp = pltpu.make_async_remote_copy(
                src_ref=nsend.at[phase], dst_ref=nrecv.at[phase * 8 + o],
                send_sem=n_ss.at[phase * 8 + o], recv_sem=n_rs.at[phase * 8 + o],
                device_id=peer, device_id_type=MESH,
            )
            cp.start()
            copies.append(cp)
        for (o, _), cp in zip(peers, copies):
            cp.wait_recv()
            message = message + nrecv[phase * 8 + o]
        sends.extend(copies)
        return message

    message = exchange(0, [(0, {"c": other})], message)
    message = exchange(1, [(o, {"tensor": lax.rem(tx + o, 8)}) for o in range(1, 8)], message)
    message = exchange(2, [(o, {"pipe": lax.rem(pz + o, 8)}) for o in range(1, 8)], message)
    message = exchange(3, [(o, {"y": lax.rem(y + o, 8)}) for o in range(1, 8)], message)
    totals = jnp.sum(message, axis=1, keepdims=True)
    rms = jnp.sqrt(totals[0:1] / ENTRIES)
    clip = jnp.minimum(1.0, 0.05 / (rms + 1e-6))
    out_drop[0] = totals[1, 0].astype(jnp.int32)

    t = jnp.full((8, 128), steps_s[0], jnp.int32)

    def power(base):
        result = jnp.ones((8, 128), jnp.float32)
        factor = jnp.full((8, 128), base, jnp.float32)
        for bit in range(5):
            result = jnp.where(((t >> bit) & 1) == 1, result * factor, result)
            factor = factor * factor
        return result

    bias1 = (1.0 - power(0.9))[0:1, 0:1]
    bias2 = (1.0 - power(0.999))[0:1, 0:1]

    for s in states:
        s.wait()
    g = mean * clip
    w = st[0]
    new_m = 0.9 * st[1] + 0.1 * g
    new_v = 0.999 * st[2] + 0.001 * g * g
    direction = (new_m / bias1) / (jnp.sqrt(new_v / bias2) + 1e-8) + 0.1 * w
    out_m[...] = new_m
    out_v[...] = new_v
    out_d[...] = direction
    out_w[...] = w - 0.001 * direction

    f_copy.wait_send()
    for cp in (*d_copies.values(), *c_copies, *sends):
        cp.wait_send()


def body(grad_parts, drop_flags, owner_order, step_count, master, moment_m, moment_v):
    block = jax.ShapeDtypeStruct((ROWS, COLS), jnp.float32)
    dma = pltpu.SemaphoreType.DMA
    vmem = pl.BlockSpec(memory_space=pltpu.VMEM)
    smem = pl.BlockSpec(memory_space=pltpu.SMEM)
    hbm = pl.BlockSpec(memory_space=pltpu.HBM)
    f32 = jnp.float32
    new_w, new_m, new_v, direction, dropped = pl.pallas_call(
        kernel,
        out_shape=(block, block, block, block, jax.ShapeDtypeStruct((1,), jnp.int32)),
        in_specs=[hbm] * 7,
        out_specs=(vmem, vmem, vmem, vmem, smem),
        scratch_shapes=[
            pltpu.SMEM((2 * Y,), jnp.int32),
            pltpu.SMEM((1,), jnp.int32),
            pltpu.VMEM((1, ROWS), jnp.int32),
            pltpu.VMEM((2 * Y, ROWS, COLS), f32),
            pltpu.VMEM((3, ROWS, COLS), f32),
            pltpu.VMEM((8, ROWS, COLS), f32),
            pltpu.VMEM((8, ROWS, COLS), f32),
            pltpu.VMEM((2, 4, ROWS, COLS), f32),
            pltpu.VMEM((2, 4, ROWS, COLS), f32),
            pltpu.VMEM((1, 128), f32),
            pltpu.VMEM((1, 128), f32),
            pltpu.VMEM((1, 128), f32),
            pltpu.VMEM((8, 1, 128), f32),
            pltpu.VMEM((4, 2, 128), f32),
            pltpu.VMEM((32, 2, 128), f32),
            dma((16,)), dma((3,)), dma((3,)), dma((8,)), dma((8,)), dma((16,)), dma((16,)),
            dma, dma, dma((8,)), dma((8,)), dma((32,)), dma((32,)),
        ],
        compiler_params=pltpu.CompilerParams(
            collective_id=0, has_side_effects=True, vmem_limit_bytes=60 * 1024 * 1024
        ),
        name="clipped_adamw",
    )(
        owner_order,
        step_count.reshape(1),
        drop_flags.reshape(1, ROWS),
        grad_parts.reshape(ROWS, WIDTH),
        master.reshape(ROWS, COLS),
        moment_m.reshape(ROWS, COLS),
        moment_v.reshape(ROWS, COLS),
    )
    shape = (1, 1, ROWS, COLS)
    return (
        new_w.reshape(shape), new_m.reshape(shape), new_v.reshape(shape),
        direction.reshape(shape), dropped.reshape(()),
    )


def solution(mesh):
    finer = Mesh(
        mesh.devices.reshape(Y, 2, mesh.shape["tensor"], mesh.shape["pipe"]),
        ("y", "c", "tensor", "pipe"),
    )
    dp = ("y", "c")
    state = P("pipe", "tensor", None, dp)
    return jax.shard_map(
        body,
        mesh=finer,
        in_specs=(
            P(dp, "pipe", "tensor", None, None), P(dp, "pipe", "tensor", None), P(), P(),
            state, state, state,
        ),
        out_specs=(state, state, state, state, P()),
        check_vma=False,
    )
```

time: 148 us -> 62.8 us (0.42)
  the two profiles are of different devices: /device:TPU:16 before, /device:TPU:1 now
where the time goes in v1:
time: 62.8 us; the launch traced here: 62.6 us
  Pallas kernels  53.3 us (85%)
  local copies, waits for them, and re-layouts  6.27 us (10%)
  between operations  2.99 us (5%)
    pallas_call x1, Pallas kernels, body(): pl.pallas_call(kernel, out_shape=(block, block, block, block, jax.ShapeDt...  53.3 us
    unnamed x4, local copies, waits for them, and re-layouts  6.27 us

profile of v1, /device:TPU:1, one launch (start us, length us, event | category | flops | bytes accessed | tf_op | source)
XLA Modules:
  0.0 62.6 jit_solution(18411579388262938984)
XLA Ops:
  1.3 53.3 %clipped_adamw.1 = (f32[64,512]{1,0:T(8,128)}, f32[64,512]{1,0:T(8,128)}, f32[64,512]{1,0:T(8,128)}, f32[64,512]{1,0:T(8,128)}, s32[1]{0:T(128)}) custom-call(s32[16]{0:T(128)} %order.1, s32[1]{0:T(128)} %bitcast.11.steps, s32[1,64]{1,0:T(1,128)} %bitcast.20, f32[64,8192]{1,0:T(8,128)} %bitcast.12, f32[64,512]{1,0:T(8,128)} %bitcast.13, f32[64,512]{1,0:T(8,128)} %bitcast.14, ...), custom_call_target="tpu_custom_call" | custom-call | tf_op jit(solution)/shard_map/clipped_adamw/pallas_call | solution.py:239
  54.6 1.6 %copy.18 = f32[1,1,64,512]{3,2,1,0:T(8,128)} copy(f32[1,1,64,512]{3,2,1,0:T(8,128)} %bitcast.19) | data formatting | bytes 262144
  56.2 1.6 %copy.19 = f32[1,1,64,512]{3,2,1,0:T(8,128)} copy(f32[1,1,64,512]{3,2,1,0:T(8,128)} %bitcast.18) | data formatting | bytes 262144
  57.7 1.6 %copy.20 = f32[1,1,64,512]{3,2,1,0:T(8,128)} copy(f32[1,1,64,512]{3,2,1,0:T(8,128)} %bitcast.17) | data formatting | bytes 262144
  59.3 1.6 %copy.21 = f32[1,1,64,512]{3,2,1,0:T(8,128)} copy(f32[1,1,64,512]{3,2,1,0:T(8,128)} %bitcast.16) | data formatting | bytes 262144

commit v2 on v1

--- a/solution.py
+++ b/solution.py
@@ -18,11 +18,13 @@
 DOWN = ((4, 1), (3, 0), (3, 1), (2, 0), (2, 1), (1, 0), (1, 1))
 
 
+PLANE_ORDER = [8 * dx + dz for dz in (1, 2, 3, 4, 5, 6, 7, 0) for dx in (4, 3, 5, 2, 6, 1, 7, 0) if dx or dz]
+
+
 def kernel(
-    order, steps, flags, grad, master, moment_m, moment_v,
-    out_w, out_m, out_v, out_d, out_drop,
-    order_s, steps_s, flags_v, x, st, dsend, drecv, ring_send, ring_recv, fsend, frecv, csend, crecv, nsend, nrecv,
-    load_sem, small_sem, st_sem, d_ss, d_rs, r_ss, r_rs, f_ss, f_rs, c_ss, c_rs, n_ss, n_rs,
+    order, steps, flags, grad, out_g, out_b1, out_b2, out_drop,
+    order_s, flags_v, x, dsend, drecv, ring_send, ring_recv, fsend, frecv, csend, crecv, lsend, lrecv, psend, precv,
+    load_sem, small_sem, d_ss, d_rs, r_ss, r_rs, f_ss, f_rs, c_ss, c_rs, n_ss, n_rs,
 ):
     y = lax.axis_index("y")
     c = lax.axis_index("c")
@@ -30,16 +32,9 @@
     pz = lax.axis_index("pipe")
     other = 1 - c
 
-    barrier = pltpu.get_barrier_semaphore()
-    pl.semaphore_signal(barrier, inc=1, device_id={"c": other}, device_id_type=MESH)
-    for o in range(1, 8):
-        pl.semaphore_signal(barrier, inc=1, device_id={"y": lax.rem(y + o, 8)}, device_id_type=MESH)
-        pl.semaphore_signal(barrier, inc=1, device_id={"tensor": lax.rem(tx + o, 8)}, device_id_type=MESH)
-        pl.semaphore_signal(barrier, inc=1, device_id={"pipe": lax.rem(pz + o, 8)}, device_id_type=MESH)
-
     smalls = [
         pltpu.make_async_copy(ref, to, small_sem.at[i])
-        for i, (ref, to) in enumerate(((flags, flags_v), (order, order_s), (steps, steps_s)))
+        for i, (ref, to) in enumerate(((flags, flags_v), (order, order_s)))
     ]
     for s in smalls:
         s.start()
@@ -49,12 +44,15 @@
     ]
     for s in loads:
         s.start()
-    states = [
-        pltpu.make_async_copy(ref, st.at[i], st_sem.at[i])
-        for i, ref in enumerate((master, moment_m, moment_v))
-    ]
-    for s in states:
-        s.start()
+    line = [{"c": other}] + [
+        {"y": lax.rem(y + o // 2, 8), "c": lax.rem(c + o % 2, 2)} for o in range(2, 16)
+    ]
+    plane = [
+        {"tensor": lax.rem(tx + o // 8, 8), "pipe": lax.rem(pz + o % 8, 8)} for o in PLANE_ORDER
+    ]
+    barrier = pltpu.get_barrier_semaphore()
+    for peer in line + plane:
+        pl.semaphore_signal(barrier, inc=1, device_id=peer, device_id_type=MESH)
 
     for s in smalls:
         s.wait()
@@ -68,6 +66,7 @@
         return jnp.sum(jnp.where(eye, jnp.broadcast_to(row, (ROWS, ROWS)), 0.0), axis=1, keepdims=True)
 
     kept = as_column(kept_row)
+    flag_lanes = jnp.concatenate([jnp.zeros((1, 64), jnp.float32), flag_row], axis=1)
     fsend[...] = jnp.concatenate([kept_row, jnp.zeros((1, 128 - ROWS), jnp.float32)], axis=1)
 
     def mine(chip, core, lo, n):
@@ -75,7 +74,7 @@
 
     for s in loads:
         s.wait()
-    pl.semaphore_wait(barrier, 22)
+    pl.semaphore_wait(barrier, 78)
 
     d_copies = {}
     for d in D_ORDER:
@@ -169,60 +168,47 @@
     squares = squares[:, 0:128] + squares[:, 128:256] + squares[:, 256:384] + squares[:, 384:512]
     squares = jnp.sum(squares, axis=0, keepdims=True)
 
-    message = jnp.concatenate(
-        [squares, jnp.concatenate([flag_row, jnp.zeros((1, 128 - ROWS), jnp.float32)], axis=1)], axis=0
-    )
-
-    def exchange(phase, peers, message):
-        nsend[phase] = message
-        copies = []
-        for o, peer in peers:
+    low = lax.broadcasted_iota(jnp.int32, (1, 128), 1) < 64
+    message = jnp.where(low, squares + pltpu.roll(squares, 64, 1), flag_lanes)
+
+    def exchange(slots, peers, message, out, into, ss, rs):
+        out[...] = message
+        into[0:1] = message
+        for o, peer in zip(slots, peers):
             cp = pltpu.make_async_remote_copy(
-                src_ref=nsend.at[phase], dst_ref=nrecv.at[phase * 8 + o],
-                send_sem=n_ss.at[phase * 8 + o], recv_sem=n_rs.at[phase * 8 + o],
+                src_ref=out, dst_ref=into.at[pl.ds(o, 1)], send_sem=ss, recv_sem=rs,
                 device_id=peer, device_id_type=MESH,
             )
             cp.start()
-            copies.append(cp)
-        for (o, _), cp in zip(peers, copies):
-            cp.wait_recv()
-            message = message + nrecv[phase * 8 + o]
-        sends.extend(copies)
-        return message
-
-    message = exchange(0, [(0, {"c": other})], message)
-    message = exchange(1, [(o, {"tensor": lax.rem(tx + o, 8)}) for o in range(1, 8)], message)
-    message = exchange(2, [(o, {"pipe": lax.rem(pz + o, 8)}) for o in range(1, 8)], message)
-    message = exchange(3, [(o, {"y": lax.rem(y + o, 8)}) for o in range(1, 8)], message)
-    totals = jnp.sum(message, axis=1, keepdims=True)
-    rms = jnp.sqrt(totals[0:1] / ENTRIES)
+        n = len(slots)
+        everything = pltpu.make_async_remote_copy(
+            src_ref=into.at[pl.ds(0, n)], dst_ref=into.at[pl.ds(0, n)], send_sem=ss, recv_sem=rs,
+            device_id=peers[0], device_id_type=MESH,
+        )
+        everything.wait_recv()
+        sends.append(everything)
+        return jnp.sum(into[...], axis=0, keepdims=True)
+
+    message = exchange(range(1, 16), line, message, lsend, lrecv, n_ss.at[0], n_rs.at[0])
+    message = exchange(PLANE_ORDER, plane, message, psend, precv, n_ss.at[1], n_rs.at[1])
+    total = jnp.sum(jnp.where(low, message, 0.0), axis=1, keepdims=True)
+    dropped = jnp.sum(jnp.where(low, 0.0, message), axis=1, keepdims=True)
+    rms = jnp.sqrt(total / ENTRIES)
     clip = jnp.minimum(1.0, 0.05 / (rms + 1e-6))
-    out_drop[0] = totals[1, 0].astype(jnp.int32)
-
-    t = jnp.full((8, 128), steps_s[0], jnp.int32)
+    out_drop[...] = dropped[0, 0].astype(jnp.int32)
+
+    t = steps[...]
 
     def power(base):
-        result = jnp.ones((8, 128), jnp.float32)
-        factor = jnp.full((8, 128), base, jnp.float32)
+        result, factor = jnp.float32(1.0), jnp.float32(base)
         for bit in range(5):
             result = jnp.where(((t >> bit) & 1) == 1, result * factor, result)
             factor = factor * factor
         return result
 
-    bias1 = (1.0 - power(0.9))[0:1, 0:1]
-    bias2 = (1.0 - power(0.999))[0:1, 0:1]
-
-    for s in states:
-        s.wait()
-    g = mean * clip
-    w = st[0]
-    new_m = 0.9 * st[1] + 0.1 * g
-    new_v = 0.999 * st[2] + 0.001 * g * g
-    direction = (new_m / bias1) / (jnp.sqrt(new_v / bias2) + 1e-8) + 0.1 * w
-    out_m[...] = new_m
-    out_v[...] = new_v
-    out_d[...] = direction
-    out_w[...] = w - 0.001 * direction
+    out_b1[...] = jnp.full((ROWS, COLS), 1.0 - power(0.9), jnp.float32)
+    out_b2[...] = jnp.full((ROWS, COLS), 1.0 - power(0.999), jnp.float32)
+    out_g[...] = mean * clip
 
     f_copy.wait_send()
     for cp in (*d_copies.values(), *c_copies, *sends):
@@ -236,17 +222,15 @@
     smem = pl.BlockSpec(memory_space=pltpu.SMEM)
     hbm = pl.BlockSpec(memory_space=pltpu.HBM)
     f32 = jnp.float32
-    new_w, new_m, new_v, direction, dropped = pl.pallas_call(
+    g, bias1, bias2, dropped = pl.pallas_call(
         kernel,
-        out_shape=(block, block, block, block, jax.ShapeDtypeStruct((1,), jnp.int32)),
-        in_specs=[hbm] * 7,
-        out_specs=(vmem, vmem, vmem, vmem, smem),
+        out_shape=(block, block, block, jax.ShapeDtypeStruct((), jnp.int32)),
+        in_specs=[hbm, smem, hbm, hbm],
+        out_specs=(vmem, vmem, vmem, smem),
         scratch_shapes=[
             pltpu.SMEM((2 * Y,), jnp.int32),
-            pltpu.SMEM((1,), jnp.int32),
             pltpu.VMEM((1, ROWS), jnp.int32),
             pltpu.VMEM((2 * Y, ROWS, COLS), f32),
-            pltpu.VMEM((3, ROWS, COLS), f32),
             pltpu.VMEM((8, ROWS, COLS), f32),
             pltpu.VMEM((8, ROWS, COLS), f32),
             pltpu.VMEM((2, 4, ROWS, COLS), f32),
@@ -255,29 +239,31 @@
             pltpu.VMEM((1, 128), f32),
             pltpu.VMEM((1, 128), f32),
             pltpu.VMEM((8, 1, 128), f32),
-            pltpu.VMEM((4, 2, 128), f32),
-            pltpu.VMEM((32, 2, 128), f32),
-            dma((16,)), dma((3,)), dma((3,)), dma((8,)), dma((8,)), dma((16,)), dma((16,)),
-            dma, dma, dma((8,)), dma((8,)), dma((32,)), dma((32,)),
+            pltpu.VMEM((1, 128), f32),
+            pltpu.VMEM((16, 128), f32),
+            pltpu.VMEM((1, 128), f32),
+            pltpu.VMEM((64, 128), f32),
+            dma((16,)), dma((2,)), dma((8,)), dma((8,)), dma((16,)), dma((16,)),
+            dma, dma, dma((8,)), dma((8,)), dma((2,)), dma((2,)),
         ],
         compiler_params=pltpu.CompilerParams(
-            collective_id=0, has_side_effects=True, vmem_limit_bytes=60 * 1024 * 1024
+            collective_id=0, has_side_effects=True, vmem_limit_bytes=16 << 20
         ),
         name="clipped_adamw",
     )(
-        owner_order,
-        step_count.reshape(1),
-        drop_flags.reshape(1, ROWS),
-        grad_parts.reshape(ROWS, WIDTH),
-        master.reshape(ROWS, COLS),
-        moment_m.reshape(ROWS, COLS),
-        moment_v.reshape(ROWS, COLS),
-    )
-    shape = (1, 1, ROWS, COLS)
-    return (
-        new_w.reshape(shape), new_m.reshape(shape), new_v.reshape(shape),
-        direction.reshape(shape), dropped.reshape(()),
-    )
+        pltpu.with_memory_space_constraint(owner_order, pltpu.HBM),
+        step_count,
+        pltpu.with_memory_space_constraint(drop_flags.reshape(1, ROWS), pltpu.HBM),
+        pltpu.with_memory_space_constraint(grad_parts.reshape(ROWS, WIDTH), pltpu.HBM),
+    )
+    g = g.reshape(master.shape)
+    new_m = 0.9 * moment_m + 0.1 * g
+    new_v = 0.999 * moment_v + 0.001 * g * g
+    m_hat = new_m / bias1.reshape(master.shape)
+    v_hat = new_v / bias2.reshape(master.shape)
+    direction = m_hat / (jnp.sqrt(v_hat) + 1e-8) + 0.1 * master
+    new_master = master - 0.001 * direction
+    return new_master, new_m, new_v, direction, dropped
 
 
 def solution(mesh):

time: 62.8 us -> 55.8 us (0.89)
  local copies, waits for them, and re-layouts: 6.27 us -> 0.01 us
  Pallas kernels: 53.3 us -> 51.6 us
  other arithmetic: 0 us -> 0.84 us
    unnamed x4 -> x6, local copies, waits for them, and re-layouts: 6.27 us -> 0.01 us
    pallas_call x1, Pallas kernels: 53.3 us -> 51.6 us  [body(): pl.pallas_call(kernel, out_shape=(block, block, block, jax.ShapeDtypeStru...]
    sub x0 -> x1, other arithmetic: none -> 0.84 us  [body(): new_master = master - 0.001 * direction]
where the time goes in v2:
time: 55.8 us; the launch traced here: 55.6 us
  Pallas kernels  51.6 us (92%)
  between operations  3.13 us (6%)
  other arithmetic  0.84 us (2%)
    pallas_call x1, Pallas kernels, body(): pl.pallas_call(kernel, out_shape=(block, block, block, jax.ShapeDtypeStru...  51.6 us

profile of v2, /device:TPU:1, one launch (start us, length us, event | category | flops | bytes accessed | tf_op | source)
XLA Modules:
  0.0 55.6 jit_solution(521652688469000551)
XLA Ops:
  0.6 0.0 copy-start.1
  0.6 0.0 copy-start.2
  0.7 0.0 copy-start
  1.4 51.6 %clipped_adamw.1 = (f32[64,512]{1,0:T(8,128)S(1)}, f32[64,512]{1,0:T(8,128)S(1)}, f32[64,512]{1,0:T(8,128)S(1)}, s32[]{:T(128)}) custom-call(s32[16]{0:T(128)} %order.1, s32[]{:T(128)S(6)} %copy.13.steps, s32[1,64]{1,0:T(1,128)} %bitcast.27, f32[64,8192]{1,0:T(8,128)} %bitcast.26), custom_call_target="tpu_custom_call" | custom-call | tf_op jit(solution)/shard_map/clipped_adamw/pallas_call | solution.py:225
  53.0 0.0 copy-done.1
  53.0 0.0 copy-done.2
  53.0 0.0 copy-done
  53.0 0.8 %multiply_subtract_fusion = (f32[1,1,64,512]{3,2,1,0:T(8,128)}, f32[1,1,64,512]{3,2,1,0:T(8,128)}, f32[1,1,64,512]{3,2,1,0:T(8,128)}, f32[1,1,64,512]{3,2,1,0:T(8,128)}) fusion(f32[1,1,64,512]{3,2,1,0:T(8,128)S(1)} %copy-done, f32[64,512]{1,0:T(8,128)S(1)} %get-tuple-element.11, f32[64,512]{1,0:T(8,128)S(1)} %get-tuple-element.10, ...), kind=kLoop, calls=%fused_computation.10 | loop fusion | flops 491520 | bytes 1310720 | tf_op jit(solution)/shard_map/sub | solution.py:265
Async XLA Ops:
  0.6 52.4 %copy-start.1 = (f32[1,1,64,512]{3,2,1,0:T(8,128)S(1)}, f32[1,1,64,512]{3,2,1,0:T(8,128)}, u32[]{:S(2)}) copy-start(f32[1,1,64,512]{3,2,1,0:T(8,128)} %param.13) | copy-start | bytes 393220
  0.6 52.4 %copy-start.2 = (f32[1,1,64,512]{3,2,1,0:T(8,128)S(1)}, f32[1,1,64,512]{3,2,1,0:T(8,128)}, u32[]{:S(2)}) copy-start(f32[1,1,64,512]{3,2,1,0:T(8,128)} %param.12) | copy-start | bytes 393220
  0.7 52.4 %copy-start = (f32[1,1,64,512]{3,2,1,0:T(8,128)S(1)}, f32[1,1,64,512]{3,2,1,0:T(8,128)}, u32[]{:S(2)}) copy-start(f32[1,1,64,512]{3,2,1,0:T(8,128)} %param.11) | copy-start | bytes 393220

commit v3 on v2

v3 whole, which is shorter than its diff:
```python
import jax
import jax.numpy as jnp
from jax import lax
from jax.experimental import pallas as pl
from jax.experimental.pallas import tpu as pltpu
from jax.sharding import Mesh
from jax.sharding import PartitionSpec as P

MESH = pl.DeviceIdType.MESH
Y = 8
ROWS, COLS = 64, 512
WIDTH = 2 * Y * COLS
PIECES = 4
PIECE = ROWS // PIECES
ENTRIES = 33554432.0

SHORT = 1 + 7 + 15 + 63

PLANE = [8 * dx + dz for dz in (1, 2, 3, 4, 5, 6, 7, 0) for dx in (4, 3, 5, 2, 6, 1, 7, 0) if dx or dz]

D_ORDER = (4, 3, 5, 2, 6, 1, 7, 0)
SLOT = {d: i for i, d in enumerate(D_ORDER)}
GROUPS = ((0, 1), (1, 2), (3, 2), (5, 2), (7, 1))
GROUP = (0, 1, 1, 2, 2, 3, 3, 4)
FIRST, SECOND = tuple(range(PIECES // 2)), tuple(range(PIECES // 2, PIECES))


def ring_order(long, short):
    order = [(4, p) for p in long]
    for k in (3, 2, 1):
        order += [(k, p) for p in short] + [(k, p) for p in long]
    return order


WAYS = (ring_order(FIRST, SECOND), ring_order(SECOND, FIRST))
LONG = (FIRST, SECOND)


def kernel(
    order, steps, flags, grad, out_g, out_b1, out_b2, out_drop,
    order_s, flags_v, x, dsend, drecv, ring_send, ring_recv, fsend, frecv, csend, crecv, lsend, lrecv, xsend, xrecv,
    tally, load_sem, small_sem, d_ss, d_rs, r_ss, r_rs, small_ss, f_rs, c_rs, n_rs, ready,
):
    y = lax.axis_index("y")
    c = lax.axis_index("c")
    tx = lax.axis_index("tensor")
    pz = lax.axis_index("pipe")
    other = 1 - c

    smalls = [
        pltpu.make_async_copy(ref, to, small_sem.at[i])
        for i, (ref, to) in enumerate(((flags, flags_v), (order, order_s)))
    ]
    for s in smalls:
        s.start()
    loads = [
        pltpu.make_async_copy(grad.at[:, pl.ds(b * COLS, COLS)], x.at[b], load_sem)
        for b in range(2 * Y)
    ]
    for s in loads:
        s.start()
    line = [{"c": other}] + [
        {"y": lax.rem(y + o // 2, 8), "c": lax.rem(c + o % 2, 2)} for o in range(2, 16)
    ]
    along_x = [{"tensor": lax.rem(tx + o, 8)} for o in range(1, 8)]
    along_z = [{"pipe": lax.rem(pz + o, 8)} for o in range(1, 8)]
    plane = [
        {"tensor": lax.rem(tx + o // 8, 8), "pipe": lax.rem(pz + o % 8, 8)} for o in PLANE
    ]
    barrier = pltpu.get_barrier_semaphore()
    for peer in line + along_x + along_z:
        pl.semaphore_signal(barrier, inc=1, device_id=peer, device_id_type=MESH)

    for s in smalls:
        s.wait()
    flag_row = flags_v[...].astype(jnp.float32)
    kept_row = 1.0 - flag_row
    eye = lax.broadcasted_iota(jnp.int32, (ROWS, ROWS), 0) == lax.broadcasted_iota(
        jnp.int32, (ROWS, ROWS), 1
    )

    def as_column(row):
        return jnp.sum(jnp.where(eye, jnp.broadcast_to(row, (ROWS, ROWS)), 0.0), axis=1, keepdims=True)

    kept = as_column(kept_row)
    flag_lanes = jnp.concatenate([jnp.zeros((1, 64), jnp.float32), flag_row], axis=1)
    fsend[...] = jnp.concatenate([kept_row, jnp.zeros((1, 128 - ROWS), jnp.float32)], axis=1)

    def mine(chip, core, lo, n):
        return x[order_s[2 * chip + core], lo : lo + n] * kept[lo : lo + n]

    pltpu.make_async_copy(x, x, load_sem).wait()
    pl.semaphore_wait(barrier, 29)
    for peer in along_x:
        pl.semaphore_signal(ready, inc=1, device_id=peer, device_id_type=MESH)

    for slot, d in enumerate(D_ORDER):
        dsend[slot] = mine(lax.rem(y + d, 8), other, 0, ROWS)
        pltpu.make_async_remote_copy(
            src_ref=dsend.at[slot], dst_ref=drecv.at[slot], send_sem=d_ss, recv_sem=d_rs.at[GROUP[slot]],
            device_id={"c": other}, device_id_type=MESH,
        ).start()
    f_copy = pltpu.make_async_remote_copy(
        src_ref=fsend, dst_ref=frecv, send_sem=small_ss, recv_sem=f_rs,
        device_id={"c": other}, device_id_type=MESH,
    )
    f_copy.start()

    def on_chip(d, piece):
        group = GROUP[SLOT[d]]
        if group not in seen:
            seen.add(group)
            slots = drecv.at[pl.ds(*GROUPS[group])]
            pltpu.make_async_remote_copy(
                src_ref=slots, dst_ref=slots, send_sem=d_ss, recv_sem=d_rs.at[group],
                device_id={"c": other}, device_id_type=MESH,
            ).wait_recv()
        lo = piece * PIECE
        return mine(lax.rem(y + d, 8), c, lo, PIECE) + drecv[SLOT[d], lo : lo + PIECE]

    seen = set()

    def ring_copy(way, k, piece):
        rows = pl.ds(piece * PIECE, PIECE)
        i = way * len(WAYS[0]) + WAYS[way].index((k, piece))
        return pltpu.make_async_remote_copy(
            src_ref=ring_send.at[way, k - 1, rows], dst_ref=ring_recv.at[way, k - 1, rows],
            send_sem=r_ss, recv_sem=r_rs.at[i],
            device_id={"y": lax.rem(y + (1 if way == 0 else 7), 8)}, device_id_type=MESH,
        )

    def stage(way, k, piece):
        lo = piece * PIECE
        value = on_chip(k if way == 0 else 8 - k, piece)
        if k < (4 if piece in LONG[way] else 3):
            ring_copy(way, k + 1, piece).wait_recv()
            value = value + ring_recv[way, k, lo : lo + PIECE]
        ring_send[way, k - 1, lo : lo + PIECE] = value
        ring_copy(way, k, piece).start()

    for i in range(len(WAYS[0])):
        stage(0, *WAYS[0][i])
        stage(1, *WAYS[1][i])
        if i == PIECES - 1:
            f_copy.wait_recv()
            csend[...] = fsend[...] + frecv[...]
            for o in range(1, 8):
                pltpu.make_async_remote_copy(
                    src_ref=csend, dst_ref=crecv.at[o], send_sem=small_ss, recv_sem=c_rs,
                    device_id={"y": lax.rem(y + o, 8)}, device_id_type=MESH,
                ).start()

    counts = crecv.at[pl.ds(1, 7)]
    pltpu.make_async_remote_copy(
        src_ref=counts, dst_ref=counts, send_sem=small_ss, recv_sem=c_rs,
        device_id={"c": other}, device_id_type=MESH,
    ).wait_recv()
    count_row = csend[...]
    for o in range(1, 8):
        count_row = count_row + crecv[o]
    count = jnp.maximum(as_column(count_row[:, :ROWS]), 1.0)

    squares = jnp.zeros((8, COLS), jnp.float32)
    means = [None] * PIECES
    for piece in (p for pair in zip(FIRST, SECOND) for p in pair):
        lo = piece * PIECE
        part = on_chip(0, piece)
        for way in ((1, 0) if piece in FIRST else (0, 1)):
            ring_copy(way, 1, piece).wait_recv()
            part = part + ring_recv[way, 0, lo : lo + PIECE]
        mean = part / count[lo : lo + PIECE]
        means[piece] = mean
        for r in range(0, PIECE, 8):
            squares = squares + mean[r : r + 8] * mean[r : r + 8]
    mean = jnp.concatenate(means, axis=0)
    squares = squares[:, 0:128] + squares[:, 128:256] + squares[:, 256:384] + squares[:, 384:512]
    squares = jnp.sum(squares, axis=0, keepdims=True)

    low = lax.broadcasted_iota(jnp.int32, (1, 128), 1) < 64
    message = jnp.where(low, squares + pltpu.roll(squares, 64, 1), flag_lanes)

    def exchange(slots, peers, message, out, into, rs):
        out[...] = message
        into[0:1] = message
        for o, peer in zip(slots, peers):
            cp = pltpu.make_async_remote_copy(
                src_ref=out, dst_ref=into.at[pl.ds(o, 1)], send_sem=small_ss, recv_sem=rs,
                device_id=peer, device_id_type=MESH,
            )
            cp.start()
        n = len(slots)
        everything = pltpu.make_async_remote_copy(
            src_ref=into.at[pl.ds(0, n)], dst_ref=into.at[pl.ds(0, n)], send_sem=small_ss, recv_sem=rs,
            device_id=peers[0], device_id_type=MESH,
        )
        everything.wait_recv()
        return jnp.sum(into[...], axis=0, keepdims=True)

    message = exchange(range(1, 16), line, message, lsend, lrecv, n_rs.at[0])
    pl.semaphore_wait(ready, 7)
    message = exchange(PLANE, plane, message, xsend, xrecv, n_rs.at[1])
    total = jnp.sum(jnp.where(low, message, 0.0), axis=1, keepdims=True)
    dropped = jnp.sum(jnp.where(low, 0.0, message), axis=1, keepdims=True)
    rms = jnp.sqrt(total / ENTRIES)
    clip = jnp.minimum(1.0, 0.05 / (rms + 1e-6))
    out_drop[...] = jnp.broadcast_to(dropped, (1, 128)).astype(jnp.int32)

    t = steps[...]

    def power(base):
        result, factor = jnp.float32(1.0), jnp.float32(base)
        for bit in range(5):
            result = jnp.where(((t >> bit) & 1) == 1, result * factor, result)
            factor = factor * factor
        return result

    out_b1[...] = jnp.full((ROWS, COLS), 1.0 - power(0.9), jnp.float32)
    out_b2[...] = jnp.full((ROWS, COLS), 1.0 - power(0.999), jnp.float32)
    out_g[...] = mean * clip

    for ref, sem in (
        (dsend, d_ss), (ring_send.at[:, :, pl.ds(0, 56)], r_ss), (tally.at[pl.ds(0, SHORT)], small_ss)
    ):
        pltpu.make_async_remote_copy(
            src_ref=ref, dst_ref=ref, send_sem=sem, recv_sem=f_rs,
            device_id={"c": other}, device_id_type=MESH,
        ).wait_send()


def body(grad_parts, drop_flags, owner_order, step_count, master, moment_m, moment_v):
    block = jax.ShapeDtypeStruct((ROWS, COLS), jnp.float32)
    dma = pltpu.SemaphoreType.DMA
    vmem = pl.BlockSpec(memory_space=pltpu.VMEM)
    smem = pl.BlockSpec(memory_space=pltpu.SMEM)
    hbm = pl.BlockSpec(memory_space=pltpu.HBM)
    f32 = jnp.float32
    g, bias1, bias2, dropped = pl.pallas_call(
        kernel,
        out_shape=(block, block, block, jax.ShapeDtypeStruct((1, 128), jnp.int32)),
        in_specs=[hbm, smem, hbm, hbm],
        out_specs=(vmem, vmem, vmem, vmem),
        scratch_shapes=[
            pltpu.SMEM((2 * Y,), jnp.int32),
            pltpu.VMEM((1, ROWS), jnp.int32),
            pltpu.VMEM((2 * Y, ROWS, COLS), f32),
            pltpu.VMEM((8, ROWS, COLS), f32),
            pltpu.VMEM((8, ROWS, COLS), f32),
            pltpu.VMEM((2, 4, ROWS, COLS), f32),
            pltpu.VMEM((2, 4, ROWS, COLS), f32),
            pltpu.VMEM((1, 128), f32),
            pltpu.VMEM((1, 128), f32),
            pltpu.VMEM((1, 128), f32),
            pltpu.VMEM((8, 1, 128), f32),
            pltpu.VMEM((1, 128), f32),
            pltpu.VMEM((16, 128), f32),
            pltpu.VMEM((1, 128), f32),
            pltpu.VMEM((64, 128), f32),
            pltpu.VMEM((SHORT + 3, 128), f32),
            dma, dma((2,)), dma, dma((5,)), dma, dma((2 * len(WAYS[0]),)), dma, dma, dma, dma((2,)),
            pltpu.SemaphoreType.REGULAR,
        ],
        compiler_params=pltpu.CompilerParams(
            collective_id=0, has_side_effects=True, vmem_limit_bytes=16 << 20
        ),
        name="clipped_adamw",
    )(
        pltpu.with_memory_space_constraint(owner_order, pltpu.HBM),
        step_count,
        pltpu.with_memory_space_constraint(drop_flags.reshape(1, ROWS), pltpu.HBM),
        pltpu.with_memory_space_constraint(grad_parts.reshape(ROWS, WIDTH), pltpu.HBM),
    )
    g = g.reshape(master.shape)
    new_m = 0.9 * moment_m + 0.1 * g
    new_v = 0.999 * moment_v + 0.001 * g * g
    m_hat = new_m / bias1.reshape(master.shape)
    v_hat = new_v / bias2.reshape(master.shape)
    direction = m_hat / (jnp.sqrt(v_hat) + 1e-8) + 0.1 * master
    new_master = master - 0.001 * direction
    return new_master, new_m, new_v, direction, dropped[0, 0]


def solution(mesh):
    finer = Mesh(
        mesh.devices.reshape(Y, 2, mesh.shape["tensor"], mesh.shape["pipe"]),
        ("y", "c", "tensor", "pipe"),
    )
    dp = ("y", "c")
    state = P("pipe", "tensor", None, dp)
    return jax.shard_map(
        body,
        mesh=finer,
        in_specs=(
            P(dp, "pipe", "tensor", None, None), P(dp, "pipe", "tensor", None), P(), P(),
            state, state, state,
        ),
        out_specs=(state, state, state, state, P()),
        check_vma=False,
    )
```

time: 55.8 us -> 52.4 us (0.939)
  Pallas kernels: 51.6 us -> 48.8 us
  between operations: 3.13 us -> 2.55 us
    pallas_call x1, Pallas kernels: 51.6 us -> 48.8 us  [body(): pl.pallas_call(kernel, out_shape=(block, block, block, jax.ShapeDtypeStru...]
where the time goes in v3:
time: 52.4 us; the launch traced here: 52.2 us
  Pallas kernels  48.8 us (93%)
  between operations  2.55 us (5%)
  other arithmetic  0.85 us (2%)
    pallas_call x1, Pallas kernels, body(): pl.pallas_call(kernel, out_shape=(block, block, block, jax.ShapeDtypeStru...  48.8 us

profile of v3, /device:TPU:1, one launch (start us, length us, event | category | flops | bytes accessed | tf_op | source)
XLA Modules:
  0.0 52.2 jit_solution(2870905935282676598)
XLA Ops:
  0.6 0.0 copy-start.1
  0.6 0.0 copy-start.2
  0.7 0.0 copy-start
  1.4 48.8 %clipped_adamw.1 = (f32[64,512]{1,0:T(8,128)S(1)}, f32[64,512]{1,0:T(8,128)S(1)}, f32[64,512]{1,0:T(8,128)S(1)}, s32[1,128]{1,0:T(1,128)S(1)}) custom-call(s32[16]{0:T(128)} %order.1, s32[]{:T(128)S(6)} %copy.13.steps, s32[1,64]{1,0:T(1,128)} %bitcast.30, f32[64,8192]{1,0:T(8,128)} %bitcast.29), custom_call_target="tpu_custom_call" | custom-call | tf_op jit(solution)/shard_map/clipped_adamw/pallas_call | solution.py:237
  50.2 0.0 copy-done.1
  50.2 0.0 copy-done.2
  50.2 0.0 copy-done
  50.2 0.8 %multiply_subtract_fusion = (f32[1,1,64,512]{3,2,1,0:T(8,128)}, f32[1,1,64,512]{3,2,1,0:T(8,128)}, f32[1,1,64,512]{3,2,1,0:T(8,128)}, f32[1,1,64,512]{3,2,1,0:T(8,128)}) fusion(f32[1,1,64,512]{3,2,1,0:T(8,128)S(1)} %copy-done, f32[64,512]{1,0:T(8,128)S(1)} %get-tuple-element.11, f32[64,512]{1,0:T(8,128)S(1)} %get-tuple-element.10, ...), kind=kLoop, calls=%fused_computation.10 | loop fusion | flops 491520 | bytes 1310720 | tf_op jit(solution)/shard_map/sub | solution.py:278
Async XLA Ops:
  0.6 49.6 %copy-start.1 = (f32[1,1,64,512]{3,2,1,0:T(8,128)S(1)}, f32[1,1,64,512]{3,2,1,0:T(8,128)}, u32[]{:S(2)}) copy-start(f32[1,1,64,512]{3,2,1,0:T(8,128)} %param.13) | copy-start | bytes 393220
  0.6 49.6 %copy-start.2 = (f32[1,1,64,512]{3,2,1,0:T(8,128)S(1)}, f32[1,1,64,512]{3,2,1,0:T(8,128)}, u32[]{:S(2)}) copy-start(f32[1,1,64,512]{3,2,1,0:T(8,128)} %param.12) | copy-start | bytes 393220
  0.7 49.6 %copy-start = (f32[1,1,64,512]{3,2,1,0:T(8,128)S(1)}, f32[1,1,64,512]{3,2,1,0:T(8,128)}, u32[]{:S(2)}) copy-start(f32[1,1,64,512]{3,2,1,0:T(8,128)} %param.11) | copy-start | bytes 393220

commit v4 on v3

--- a/solution.py
+++ b/solution.py
@@ -16,6 +16,8 @@
 
 SHORT = 1 + 7 + 15 + 63
 
+LINE = [2 * dy + dc for dy in (4, 3, 5, 2, 6, 1, 7, 0) for dc in (0, 1) if dy or dc]
+
 PLANE = [8 * dx + dz for dz in (1, 2, 3, 4, 5, 6, 7, 0) for dx in (4, 3, 5, 2, 6, 1, 7, 0) if dx or dz]
 
 D_ORDER = (4, 3, 5, 2, 6, 1, 7, 0)
@@ -38,7 +40,7 @@
 
 def kernel(
     order, steps, flags, grad, out_g, out_b1, out_b2, out_drop,
-    order_s, flags_v, x, dsend, drecv, ring_send, ring_recv, fsend, frecv, csend, crecv, lsend, lrecv, xsend, xrecv,
+    order_s, flags_v, x, dsend, drecv, ring_send, ring_recv, fsend, frecv, csend, cpass, crecv, lsend, lrecv, xsend, xrecv,
     tally, load_sem, small_sem, d_ss, d_rs, r_ss, r_rs, small_ss, f_rs, c_rs, n_rs, ready,
 ):
     y = lax.axis_index("y")
@@ -59,16 +61,15 @@
     ]
     for s in loads:
         s.start()
-    line = [{"c": other}] + [
-        {"y": lax.rem(y + o // 2, 8), "c": lax.rem(c + o % 2, 2)} for o in range(2, 16)
-    ]
+    line = [{"y": lax.rem(y + o // 2, 8), "c": lax.rem(c + o % 2, 2)} for o in LINE]
     along_x = [{"tensor": lax.rem(tx + o, 8)} for o in range(1, 8)]
-    along_z = [{"pipe": lax.rem(pz + o, 8)} for o in range(1, 8)]
+    beside_y = [{"y": lax.rem(y + o, 8)} for o in (1, 7)]
+    beside_z = [{"pipe": lax.rem(pz + o, 8)} for o in (1, 7)]
     plane = [
         {"tensor": lax.rem(tx + o // 8, 8), "pipe": lax.rem(pz + o % 8, 8)} for o in PLANE
     ]
     barrier = pltpu.get_barrier_semaphore()
-    for peer in line + along_x + along_z:
+    for peer in beside_y + [{"c": other}] + beside_z + along_x:
         pl.semaphore_signal(barrier, inc=1, device_id=peer, device_id_type=MESH)
 
     for s in smalls:
@@ -90,9 +91,19 @@
         return x[order_s[2 * chip + core], lo : lo + n] * kept[lo : lo + n]
 
     pltpu.make_async_copy(x, x, load_sem).wait()
-    pl.semaphore_wait(barrier, 29)
-    for peer in along_x:
-        pl.semaphore_signal(ready, inc=1, device_id=peer, device_id_type=MESH)
+    pl.semaphore_wait(barrier, 12)
+
+    def tell(peers, i):
+        for peer in peers:
+            pl.semaphore_signal(ready.at[i], inc=1, device_id=peer, device_id_type=MESH)
+
+    tell(beside_z, 0)
+
+    f_copy = pltpu.make_async_remote_copy(
+        src_ref=fsend, dst_ref=frecv, send_sem=small_ss, recv_sem=f_rs,
+        device_id={"c": other}, device_id_type=MESH,
+    )
+    f_copy.start()
 
     for slot, d in enumerate(D_ORDER):
         dsend[slot] = mine(lax.rem(y + d, 8), other, 0, ROWS)
@@ -100,12 +111,6 @@
             src_ref=dsend.at[slot], dst_ref=drecv.at[slot], send_sem=d_ss, recv_sem=d_rs.at[GROUP[slot]],
             device_id={"c": other}, device_id_type=MESH,
         ).start()
-    f_copy = pltpu.make_async_remote_copy(
-        src_ref=fsend, dst_ref=frecv, send_sem=small_ss, recv_sem=f_rs,
-        device_id={"c": other}, device_id_type=MESH,
-    )
-    f_copy.start()
-
     def on_chip(d, piece):
         group = GROUP[SLOT[d]]
         if group not in seen:
@@ -129,6 +134,13 @@
             device_id={"y": lax.rem(y + (1 if way == 0 else 7), 8)}, device_id_type=MESH,
         )
 
+    def count_copy(way, k):
+        return pltpu.make_async_remote_copy(
+            src_ref=cpass.at[way, k - 1], dst_ref=crecv.at[way, k - 1],
+            send_sem=small_ss, recv_sem=c_rs.at[way * 4 + k - 1],
+            device_id={"y": lax.rem(y + (1 if way == 0 else 7), 8)}, device_id_type=MESH,
+        )
+
     def stage(way, k, piece):
         lo = piece * PIECE
         value = on_chip(k if way == 0 else 8 - k, piece)
@@ -137,27 +149,43 @@
             value = value + ring_recv[way, k, lo : lo + PIECE]
         ring_send[way, k - 1, lo : lo + PIECE] = value
         ring_copy(way, k, piece).start()
-
-    for i in range(len(WAYS[0])):
+        if piece == 0:
+            kept_rows = csend[...]
+            if k < 4 - way:
+                count_copy(way, k + 1).wait_recv()
+                kept_rows = kept_rows + crecv[way, k]
+            cpass[way, k - 1] = kept_rows
+            count_copy(way, k).start()
+
+    t = steps[...]
+
+    def power(base):
+        result, factor = jnp.float32(1.0), jnp.float32(base)
+        for bit in range(5):
+            result = jnp.where(((t >> bit) & 1) == 1, result * factor, result)
+            factor = factor * factor
+        return result
+
+    def bias(out, base):
+        out[...] = jnp.full((ROWS, COLS), 1.0 - power(base), jnp.float32)
+
+    f_copy.wait_recv()
+    csend[...] = fsend[...] + frecv[...]
+    rounds = len(WAYS[0])
+    for i in range(rounds):
         stage(0, *WAYS[0][i])
         stage(1, *WAYS[1][i])
-        if i == PIECES - 1:
-            f_copy.wait_recv()
-            csend[...] = fsend[...] + frecv[...]
-            for o in range(1, 8):
-                pltpu.make_async_remote_copy(
-                    src_ref=csend, dst_ref=crecv.at[o], send_sem=small_ss, recv_sem=c_rs,
-                    device_id={"y": lax.rem(y + o, 8)}, device_id_type=MESH,
-                ).start()
-
-    counts = crecv.at[pl.ds(1, 7)]
-    pltpu.make_async_remote_copy(
-        src_ref=counts, dst_ref=counts, send_sem=small_ss, recv_sem=c_rs,
-        device_id={"c": other}, device_id_type=MESH,
-    ).wait_recv()
-    count_row = csend[...]
-    for o in range(1, 8):
-        count_row = count_row + crecv[o]
+        if i == PIECES:
+            bias(out_b1, 0.9)
+            bias(out_b2, 0.999)
+        if i >= rounds - 3:
+            step = i - (rounds - 3)
+            pl.semaphore_wait(ready.at[step], 2)
+            tell(along_x if step == 2 else beside_z, step + 1)
+
+    count_copy(0, 1).wait_recv()
+    count_copy(1, 1).wait_recv()
+    count_row = csend[...] + crecv[0, 0] + crecv[1, 0]
     count = jnp.maximum(as_column(count_row[:, :ROWS]), 1.0)
 
     squares = jnp.zeros((8, COLS), jnp.float32)
@@ -196,8 +224,8 @@
         everything.wait_recv()
         return jnp.sum(into[...], axis=0, keepdims=True)
 
-    message = exchange(range(1, 16), line, message, lsend, lrecv, n_rs.at[0])
-    pl.semaphore_wait(ready, 7)
+    message = exchange(LINE, line, message, lsend, lrecv, n_rs.at[0])
+    pl.semaphore_wait(ready.at[3], 7)
     message = exchange(PLANE, plane, message, xsend, xrecv, n_rs.at[1])
     total = jnp.sum(jnp.where(low, message, 0.0), axis=1, keepdims=True)
     dropped = jnp.sum(jnp.where(low, 0.0, message), axis=1, keepdims=True)
@@ -205,17 +233,6 @@
     clip = jnp.minimum(1.0, 0.05 / (rms + 1e-6))
     out_drop[...] = jnp.broadcast_to(dropped, (1, 128)).astype(jnp.int32)
 
-    t = steps[...]
-
-    def power(base):
-        result, factor = jnp.float32(1.0), jnp.float32(base)
-        for bit in range(5):
-            result = jnp.where(((t >> bit) & 1) == 1, result * factor, result)
-            factor = factor * factor
-        return result
-
-    out_b1[...] = jnp.full((ROWS, COLS), 1.0 - power(0.9), jnp.float32)
-    out_b2[...] = jnp.full((ROWS, COLS), 1.0 - power(0.999), jnp.float32)
     out_g[...] = mean * clip
 
     for ref, sem in (
@@ -250,14 +267,15 @@
             pltpu.VMEM((1, 128), f32),
             pltpu.VMEM((1, 128), f32),
             pltpu.VMEM((1, 128), f32),
-            pltpu.VMEM((8, 1, 128), f32),
+            pltpu.VMEM((2, 4, 1, 128), f32),
+            pltpu.VMEM((2, 4, 1, 128), f32),
             pltpu.VMEM((1, 128), f32),
             pltpu.VMEM((16, 128), f32),
             pltpu.VMEM((1, 128), f32),
             pltpu.VMEM((64, 128), f32),
             pltpu.VMEM((SHORT + 3, 128), f32),
-            dma, dma((2,)), dma, dma((5,)), dma, dma((2 * len(WAYS[0]),)), dma, dma, dma, dma((2,)),
-            pltpu.SemaphoreType.REGULAR,
+            dma, dma((2,)), dma, dma((5,)), dma, dma((2 * len(WAYS[0]),)), dma, dma, dma((8,)), dma((2,)),
+            pltpu.SemaphoreType.REGULAR((4,)),
         ],
         compiler_params=pltpu.CompilerParams(
             collective_id=0, has_side_effects=True, vmem_limit_bytes=16 << 20

time: 52.4 us -> 51.4 us (0.981)
  Pallas kernels: 48.8 us -> 47.8 us
    pallas_call x1, Pallas kernels: 48.8 us -> 47.8 us  [body(): pl.pallas_call(kernel, out_shape=(block, block, block, jax.ShapeDtypeStru...]
where the time goes in v4:
time: 51.4 us; the launch traced here: 51.2 us
  Pallas kernels  47.8 us (93%)
  between operations  2.55 us (5%)
  other arithmetic  0.85 us (2%)
    pallas_call x1, Pallas kernels, body(): pl.pallas_call(kernel, out_shape=(block, block, block, jax.ShapeDtypeStru...  47.8 us

profile of v4, /device:TPU:1, one launch (start us, length us, event | category | flops | bytes accessed | tf_op | source)
XLA Modules:
  0.0 51.2 jit_solution(8536179724461779658)
XLA Ops:
  0.6 0.0 copy-start.1
  0.6 0.0 copy-start.2
  0.7 0.0 copy-start
  1.4 47.8 %clipped_adamw.1 = (f32[64,512]{1,0:T(8,128)S(1)}, f32[64,512]{1,0:T(8,128)S(1)}, f32[64,512]{1,0:T(8,128)S(1)}, s32[1,128]{1,0:T(1,128)S(1)}) custom-call(s32[16]{0:T(128)} %order.1, s32[]{:T(128)S(6)} %copy.13.steps, s32[1,64]{1,0:T(1,128)} %bitcast.30, f32[64,8192]{1,0:T(8,128)} %bitcast.29), custom_call_target="tpu_custom_call" | custom-call | tf_op jit(solution)/shard_map/clipped_adamw/pallas_call | solution.py:254
  49.2 0.0 copy-done.1
  49.2 0.0 copy-done.2
  49.2 0.0 copy-done
  49.2 0.8 %multiply_subtract_fusion = (f32[1,1,64,512]{3,2,1,0:T(8,128)}, f32[1,1,64,512]{3,2,1,0:T(8,128)}, f32[1,1,64,512]{3,2,1,0:T(8,128)}, f32[1,1,64,512]{3,2,1,0:T(8,128)}) fusion(f32[1,1,64,512]{3,2,1,0:T(8,128)S(1)} %copy-done, f32[64,512]{1,0:T(8,128)S(1)} %get-tuple-element.11, f32[64,512]{1,0:T(8,128)S(1)} %get-tuple-element.10, ...), kind=kLoop, calls=%fused_computation.10 | loop fusion | flops 491520 | bytes 1310720 | tf_op jit(solution)/shard_map/sub | solution.py:296
Async XLA Ops:
  0.6 48.5 %copy-start.1 = (f32[1,1,64,512]{3,2,1,0:T(8,128)S(1)}, f32[1,1,64,512]{3,2,1,0:T(8,128)}, u32[]{:S(2)}) copy-start(f32[1,1,64,512]{3,2,1,0:T(8,128)} %param.13) | copy-start | bytes 393220
  0.6 48.5 %copy-start.2 = (f32[1,1,64,512]{3,2,1,0:T(8,128)S(1)}, f32[1,1,64,512]{3,2,1,0:T(8,128)}, u32[]{:S(2)}) copy-start(f32[1,1,64,512]{3,2,1,0:T(8,128)} %param.12) | copy-start | bytes 393220
  0.7 48.5 %copy-start = (f32[1,1,64,512]{3,2,1,0:T(8,128)S(1)}, f32[1,1,64,512]{3,2,1,0:T(8,128)}, u32[]{:S(2)}) copy-start(f32[1,1,64,512]{3,2,1,0:T(8,128)} %param.11) | copy-start | bytes 393220
